TPU v7x, 32 devices: a whole 2x2x4 slice. The times are simulated.
32 devices in a mesh: row: 4 (over z), col: 8 (over y, x, core).
Axes of the slice: x: 2, y: 2, z: 4, core: 2. Of those that a mesh axis runs over, the one named last changes fastest.
Arguments:
- tile_data: bfloat16 [8, 4, 8, 2, 128, 128], P(None, 'row', 'col'), may hold values from 0 to 1, as said below
- tile_cols: int32 [8, 4, 8, 2], P(None, 'row', 'col'), may hold values from -1 to 31, as said below
Outputs:
- vertex_triangles: float32 [8, 4, 128], P(None, 'row', 'col')
- triangles: float32 [], replicated
Inputs may be any that keep to these rules, and one draw needn't show every extreme that they name: `tile_cols`: slot (a, r, c, s) holds -1 (empty) or a tile column J with J % 8 == c and J >= a 4 + r; the columns of one tile row are distinct; every slot of tile row 0 is filled; tile row I keeps each slot that has an allowed column with probability (32 - I) / 32, so rows with a lower index hold more tiles on average. `tile_data`: entries are 0 or 1; tiles of empty slots are zero; a tile whose column equals its tile row is strictly upper triangular; about one entry in 8 of a stored tile is 1, with edges clustered among groups of vertices.
All inputs are finite; a program needn't handle non-finite values.
Results may differ from a plain program's by a relative error of at most 0.0003.
Values may be sent and summed in bfloat16 or wider, within the bound.
A program may use at most 128 MiB of HBM per device.

v0:
```python
import jax
import jax.numpy as jnp
from jax import lax
from jax.sharding import PartitionSpec as P

vertex_scale = 2.0 ** (-14)
total_scale = 2.0 ** (-12)


def taken_in(share, axis, dim):

    def gathered(part):
        return lax.all_gather(part, axis, axis=dim, tiled=True)

    return jax.tree.map(gathered, share)


def tile_counts(stored, middle, own_tiles, own_cols, col_tiles, col_index):
    valid = middle >= 0
    clipped = jnp.clip(middle, 0, col_tiles.shape[0] - 1).astype(jnp.int32)
    partner = col_tiles[clipped]
    partner_cols = col_index[clipped]
    matches = partner_cols[:, :, None] == own_cols[None, None, :]
    matches = matches & valid[:, None, None] & (own_cols >= 0)[None, None, :]
    weights = matches.astype(jnp.bfloat16)
    targets = jnp.einsum("pqs,sxz->pqxz", weights, own_tiles, preferred_element_type=jnp.float32)
    paths = jnp.einsum("pxy,pqyz->pqxz", stored, partner, preferred_element_type=jnp.float32)
    return jnp.sum(paths * targets, axis=(0, 1, 3))


def on_device(tile_data, tile_cols):
    rows_here = tile_data.shape[0]
    slots = tile_data.shape[3]
    width = tile_data.shape[4]
    own_tiles = tile_data[:, 0, 0]
    own_cols = tile_cols[:, 0, 0]
    row_index = lax.all_gather(tile_cols, "col", axis=2, tiled=True)
    col_index = lax.all_gather(tile_cols, "row", axis=1, tiled=True)
    col_tiles = lax.all_gather(tile_data, "row", axis=1, tiled=True)
    tile_rows = col_index.shape[0] * col_index.shape[1]
    col_index = col_index.reshape(tile_rows, slots)
    col_tiles = col_tiles.reshape(tile_rows, slots, width, width)

    def add_piece(carry, piece, start):
        devices_here = piece.shape[2]
        middle = lax.dynamic_slice_in_dim(row_index, start.astype(jnp.int32), devices_here, 2)
        middle = middle.reshape(rows_here, devices_here * slots)
        stored = piece.reshape(rows_here, devices_here * slots, width, width)

        def per_row(packed):
            return tile_counts(packed[0], packed[1], packed[2], packed[3], col_tiles, col_index)

        return carry + lax.map(per_row, (stored, middle, own_tiles, own_cols))

    initial = jnp.zeros((rows_here, width), jnp.float32)
    partial_value = add_piece(initial, taken_in(tile_data, "col", 2), jnp.int32(0))
    shares = lax.psum_scatter(
        partial_value.reshape(rows_here, 1, width), "col", scatter_dimension=2, tiled=True
    )
    vertices = tile_rows * width
    overall = lax.psum(jnp.sum(partial_value), ("row", "col"))
    return (shares * vertex_scale, overall * (total_scale / vertices))


def solution(mesh):
    return jax.shard_map(
        on_device,
        mesh=mesh,
        in_specs=(P(None, "row", "col", None, None, None), P(None, "row", "col", None)),
        out_specs=(P(None, "row", "col"), P()),
        check_vma=False,
    )
```

profile of v0, /device:TPU:0, one launch (start us, length us, event | category | flops | bytes accessed | tf_op | source)
XLA Modules:
  0.0 213.5 jit_solution(9713125407251959521)
XLA Ops:
  8.7 2.4 %copy.37 = bf16[8,1,1,2,128,128]{5,3,4,0,2,1:T(2,128)(2,1)} copy(bf16[8,1,1,2,128,128]{5,4,3,2,1,0:T(8,128)(2,1)} %param.4) | data formatting | bytes 1048576 | tf_op args[0]
  11.1 12.7 %all_gather.15 = s32[8,4,1,2]{0,3,2,1:T(2,128)S(1)} all-gather(s32[8,1,1,2]{0,3,2,1:T(2,128)S(1)} %copy-done.1), channel_id=1, replica_groups=mesh['row'=4,'col'=8] {'row'}, dimensions={1}, use_global_device_ids=true | all-gather | bytes 320 | tf_op jit(solution)/shard_map/all_gather | solution.py:38
  23.9 8.8 %all_gather.12 = s32[8,1,8,2]{0,3,1,2:T(2,128)S(1)} all-gather(s32[8,1,1,2]{0,3,1,2:T(2,128)S(1)} %bitcast.68), channel_id=1, replica_groups=mesh['row'=4,'col'=8] {'col'}, dimensions={2}, use_global_device_ids=true | all-gather | bytes 576 | tf_op jit(solution)/shard_map/all_gather | solution.py:37
  32.9 24.9 %all-gather.3.cloned.1.call-done = bf16[8,4,1,2,128,128]{5,4,3,2,1,0:T(8,128)(2,1)} async-done(((bf16[8,1,1,2,128,128]{5,4,3,2,1,0:T(8,128)(2,1)}), bf16[8,4,1,2,128,128]{5,4,3,2,1,0:T(8,128)(2,1)}) %all-gather.3.cloned.1.call-update) | async-done | bytes 2097168 | tf_op jit(solution)/shard_map/all_gather | solution.py:39
  57.8 37.3 %all-gather.5.cloned.1.call-done = bf16[8,1,8,2,128,128]{5,4,3,2,1,0:T(8,128)(2,1)} async-done(((bf16[8,1,1,2,128,128]{5,4,3,2,1,0:T(8,128)(2,1)}), bf16[8,1,8,2,128,128]{5,4,3,2,1,0:T(8,128)(2,1)}) %all-gather.5.cloned.1.call-update) | async-done | bytes 4194320 | tf_op jit(solution)/shard_map/all_gather | solution.py:13
  95.1 67.3 %while.10 = (s32[]{:T(128)}, f32[8,128]{1,0:T(8,128)S(1)}, s32[8,16]{1,0:T(8,128)S(1)}, bf16[32,2,128,128]{3,2,1,0:T(8,128)(2,1)}, bf16[8,16,128,128]{3,2,1,0:T(...) while((s32[]{:T(128)}, f32[8,128]{1,0:T(8,128)S(1)}, ...), condition=%wide.region_2.3_spmd, body=%wide.region_0.2_spmd.sunk | while | flops 137364624 | bytes 20520652 | solution.py:53
  99.1 2.5 %gather_fusion.1 = bf16[16,2,128,128]{3,2,1,0:T(8,128)(2,1)S(1)} fusion(bf16[32,2,128,128]{3,2,1,0:T(8,128)(2,1)} %get-tuple-element.163, s32[1024]{0:T(1024)S(1)} %pad_clamp_fusion.2), kind=kCustom, calls=%fused_computation.clone.1 | custom fusion | bytes 2097216 | tf_op jit(solution)/shard_map/while/body/eval_jaxpr/gather | solution.py:21
  101.6 1.9 fusion.33
  107.5 2.5 %gather_fusion.1 = bf16[16,2,128,128]{3,2,1,0:T(8,128)(2,1)S(1)} fusion(bf16[32,2,128,128]{3,2,1,0:T(8,128)(2,1)} %get-tuple-element.163, s32[1024]{0:T(1024)S(1)} %pad_clamp_fusion.2), kind=kCustom, calls=%fused_computation.clone.1 | custom fusion | bytes 2097216 | tf_op jit(solution)/shard_map/while/body/eval_jaxpr/gather | solution.py:21
  110.0 1.9 fusion.33
  115.9 2.5 %gather_fusion.1 = bf16[16,2,128,128]{3,2,1,0:T(8,128)(2,1)S(1)} fusion(bf16[32,2,128,128]{3,2,1,0:T(8,128)(2,1)} %get-tuple-element.163, s32[1024]{0:T(1024)S(1)} %pad_clamp_fusion.2), kind=kCustom, calls=%fused_computation.clone.1 | custom fusion | bytes 2097216 | tf_op jit(solution)/shard_map/while/body/eval_jaxpr/gather | solution.py:21
  118.4 1.9 fusion.33
  122.5 1.8 copy.41
  124.3 2.5 %gather_fusion.1 = bf16[16,2,128,128]{3,2,1,0:T(8,128)(2,1)S(1)} fusion(bf16[32,2,128,128]{3,2,1,0:T(8,128)(2,1)} %get-tuple-element.163, s32[1024]{0:T(1024)S(1)} %pad_clamp_fusion.2), kind=kCustom, calls=%fused_computation.clone.1 | custom fusion | bytes 2097216 | tf_op jit(solution)/shard_map/while/body/eval_jaxpr/gather | solution.py:21
  126.8 1.9 fusion.33
  132.7 2.5 %gather_fusion.1 = bf16[16,2,128,128]{3,2,1,0:T(8,128)(2,1)S(1)} fusion(bf16[32,2,128,128]{3,2,1,0:T(8,128)(2,1)} %get-tuple-element.163, s32[1024]{0:T(1024)S(1)} %pad_clamp_fusion.2), kind=kCustom, calls=%fused_computation.clone.1 | custom fusion | bytes 2097216 | tf_op jit(solution)/shard_map/while/body/eval_jaxpr/gather | solution.py:21
  135.2 1.9 fusion.33
  141.1 2.5 %gather_fusion.1 = bf16[16,2,128,128]{3,2,1,0:T(8,128)(2,1)S(1)} fusion(bf16[32,2,128,128]{3,2,1,0:T(8,128)(2,1)} %get-tuple-element.163, s32[1024]{0:T(1024)S(1)} %pad_clamp_fusion.2), kind=kCustom, calls=%fused_computation.clone.1 | custom fusion | bytes 2097216 | tf_op jit(solution)/shard_map/while/body/eval_jaxpr/gather | solution.py:21
  143.6 1.9 fusion.33
  149.5 2.5 %gather_fusion.1 = bf16[16,2,128,128]{3,2,1,0:T(8,128)(2,1)S(1)} fusion(bf16[32,2,128,128]{3,2,1,0:T(8,128)(2,1)} %get-tuple-element.163, s32[1024]{0:T(1024)S(1)} %pad_clamp_fusion.2), kind=kCustom, calls=%fused_computation.clone.1 | custom fusion | bytes 2097216 | tf_op jit(solution)/shard_map/while/body/eval_jaxpr/gather | solution.py:21
  152.0 1.9 fusion.33
  157.9 2.5 %gather_fusion.1 = bf16[16,2,128,128]{3,2,1,0:T(8,128)(2,1)S(1)} fusion(bf16[32,2,128,128]{3,2,1,0:T(8,128)(2,1)} %get-tuple-element.163, s32[1024]{0:T(1024)S(1)} %pad_clamp_fusion.2), kind=kCustom, calls=%fused_computation.clone.1 | custom fusion | bytes 2097216 | tf_op jit(solution)/shard_map/while/body/eval_jaxpr/gather | solution.py:21
  160.4 1.9 fusion.33
  164.1 39.5 %psum.7 = f32[]{:T(128)} all-reduce(f32[]{:T(128)} %reduce_sum.18), channel_id=1, replica_groups=mesh['row'=4,'col'=8] {'row','col'}, use_global_device_ids=true, to_apply=%region_5.6 | all-reduce | flops 1 | bytes 8 | tf_op jit(solution)/shard_map/psum | solution.py:61
  (106 shorter events, 35.2 us)
Async XLA Ops:
  7.2 4.0 %copy-start.1 = (s32[8,1,1,2]{0,3,2,1:T(2,128)S(1)}, s32[8,1,1,2]{0,3,2,1:T(2,128)}, u32[]{:S(2)}) copy-start(s32[8,1,1,2]{0,3,2,1:T(2,128)} %param.5) | copy-start | bytes 196
  7.2 50.6 %all-gather.3.cloned.1.call-start = ((), (), s32[]{:S(2)}) async-start(), calls=%async_computation.1 | async-start | bytes 2621440 | tf_op jit(solution)/shard_map/all_gather | solution.py:39
  7.9 87.2 %all-gather.5.cloned.1.call-start = ((), (), s32[]{:S(2)}) async-start(), calls=%async_computation.2 | async-start | bytes 4718592 | tf_op jit(solution)/shard_map/all_gather | solution.py:13
  8.7 195.6 %reduce-scatter.4.cloned.1.call-start = ((), (), s32[]{:S(2)}) async-start(), calls=%async_computation.3 | async-start | bytes 73728
  99.1 2.5 %copy-start = (f32[16,2,128,128]{2,3,1,0:T(8,128)S(1)}, f32[16,2,128,128]{2,3,1,0:T(8,128)}, u32[]{:S(2)}) copy-start(f32[16,2,128,128]{2,3,1,0:T(8,128)} %copy.41) | copy-start | bytes 6291460 | tf_op jit(solution)/shard_map/while
  107.5 2.5 %copy-start = (f32[16,2,128,128]{2,3,1,0:T(8,128)S(1)}, f32[16,2,128,128]{2,3,1,0:T(8,128)}, u32[]{:S(2)}) copy-start(f32[16,2,128,128]{2,3,1,0:T(8,128)} %copy.41) | copy-start | bytes 6291460 | tf_op jit(solution)/shard_map/while
  115.9 2.5 %copy-start = (f32[16,2,128,128]{2,3,1,0:T(8,128)S(1)}, f32[16,2,128,128]{2,3,1,0:T(8,128)}, u32[]{:S(2)}) copy-start(f32[16,2,128,128]{2,3,1,0:T(8,128)} %copy.41) | copy-start | bytes 6291460 | tf_op jit(solution)/shard_map/while
  124.3 2.5 %copy-start = (f32[16,2,128,128]{2,3,1,0:T(8,128)S(1)}, f32[16,2,128,128]{2,3,1,0:T(8,128)}, u32[]{:S(2)}) copy-start(f32[16,2,128,128]{2,3,1,0:T(8,128)} %copy.41) | copy-start | bytes 6291460 | tf_op jit(solution)/shard_map/while
  132.7 2.5 %copy-start = (f32[16,2,128,128]{2,3,1,0:T(8,128)S(1)}, f32[16,2,128,128]{2,3,1,0:T(8,128)}, u32[]{:S(2)}) copy-start(f32[16,2,128,128]{2,3,1,0:T(8,128)} %copy.41) | copy-start | bytes 6291460 | tf_op jit(solution)/shard_map/while
  141.1 2.5 %copy-start = (f32[16,2,128,128]{2,3,1,0:T(8,128)S(1)}, f32[16,2,128,128]{2,3,1,0:T(8,128)}, u32[]{:S(2)}) copy-start(f32[16,2,128,128]{2,3,1,0:T(8,128)} %copy.41) | copy-start | bytes 6291460 | tf_op jit(solution)/shard_map/while
  149.5 2.5 %copy-start = (f32[16,2,128,128]{2,3,1,0:T(8,128)S(1)}, f32[16,2,128,128]{2,3,1,0:T(8,128)}, u32[]{:S(2)}) copy-start(f32[16,2,128,128]{2,3,1,0:T(8,128)} %copy.41) | copy-start | bytes 6291460 | tf_op jit(solution)/shard_map/while
  157.9 2.5 %copy-start = (f32[16,2,128,128]{2,3,1,0:T(8,128)S(1)}, f32[16,2,128,128]{2,3,1,0:T(8,128)}, u32[]{:S(2)}) copy-start(f32[16,2,128,128]{2,3,1,0:T(8,128)} %copy.41) | copy-start | bytes 6291460 | tf_op jit(solution)/shard_map/while
Sparse Core Ops, SparseCore 0:
  9.6 48.1 all-gather.2
  59.7 35.3 all-gather.4
  163.6 33.5 reduce-scatter.3
where the time goes:
time: 215 us; the launch traced here: 213 us
  waiting for transfers between devices  63.6 us (30%)
  blocking collectives  61 us (28%)
  local copies, waits for them, and re-layouts  44.8 us (21%)
  matrix products  26.4 us (12%)
  between operations  15.6 us (7%)
    psum x1, blocking collectives, on_device(): overall = lax.psum(jnp.sum(partial_value), ('row', 'col'))  39.5 us
    all_gather x1, waiting for transfers between devices, gathered(): return lax.all_gather(part, axis, axis=dim, tiled=True)  37.3 us
    all_gather x1, waiting for transfers between devices, on_device(): col_tiles = lax.all_gather(tile_data, 'row', axis=1, tiled=True)  24.9 us
    gather x8, local copies, waits for them, and re-layouts, tile_counts(): partner = col_tiles[clipped]  19.9 us
    dot_general x8, matrix products, tile_counts(): jnp.einsum('pxy,pqyz->pqxz', stored, partner, preferred_element_type=jnp....  14.9 us
    dot_general x8, local copies, waits for them, and re-layouts, tile_counts(): jnp.einsum('pqs,sxz->pqxz', weights, own_tiles, preferred_element_type=jn...  14.7 us
    all_gather x1, blocking collectives, on_device(): col_index = lax.all_gather(tile_cols, 'row', axis=1, tiled=True)  12.7 us
    dot_general x8, matrix products, tile_counts(): jnp.einsum('pqs,sxz->pqxz', weights, own_tiles, preferred_element_type=jn...  11.5 us
  transfers between devices with their start and end apart: 3, of which 2 were waited for; matrix products, arithmetic and copies ran while one was open for 2% of the time, Pallas kernels for 0%

commit v1 on v0

v1 whole, which is shorter than its diff:
```python
import functools
import math

import jax
import jax.numpy as jnp
from jax import lax
from jax.experimental import pallas as pl
from jax.experimental.pallas import tpu as pltpu
from jax.sharding import PartitionSpec as P

MESH = pl.DeviceIdType.MESH
vertex_scale = 2.0 ** (-14)
total_scale = 2.0 ** (-12)


def plane_shape(n_col):
    chips = n_col // 2
    side = math.isqrt(chips)
    return (side, side) if side * side == chips else (1, chips)


def kernel(n_row, n_col, tiles, cols_ref, plane_ref, total_ref,
           row_buf, col_buf, row_idx, col_idx, row_smem, col_smem, acc, parts, planes,
           load_sem, smem_sem, row_send, row_recv, col_send, col_recv,
           idx_send, idx_recv, part_send, part_recv, plane_send, plane_recv):
    r = lax.axis_index("row")
    c = lax.axis_index("col")
    n_tiles = tiles.shape[0]
    half = n_tiles // 2
    rows = acc.shape[0]
    slots = n_tiles // rows
    width = tiles.shape[1]
    zero = n_col * n_tiles
    Y, X = plane_shape(n_col)
    u = c % 2
    x = (c // 2) % X
    y = c // (2 * X)

    def col_of(yy, xx, uu):
        return (yy * X + xx) * 2 + uu

    def row_block(cc, h):
        return row_buf.at[pl.ds(cc * n_tiles + h * half, half)]

    def col_block(rr):
        return col_buf.at[pl.ds(rr * n_tiles, n_tiles)]

    load_row = pltpu.make_async_copy(tiles, row_buf.at[pl.ds(c * n_tiles, n_tiles)], load_sem.at[0])
    load_row.start()
    load_col = pltpu.make_async_copy(tiles, col_block(r), load_sem.at[1])
    load_col.start()
    load_ri = pltpu.make_async_copy(cols_ref, row_idx.at[c], load_sem.at[2])
    load_ri.start()
    load_ci = pltpu.make_async_copy(cols_ref, col_idx.at[r], load_sem.at[3])
    load_ci.start()

    barrier = pltpu.get_barrier_semaphore()
    for t in range(1, n_col):
        pl.semaphore_signal(barrier, inc=1, device_id={"col": lax.rem(c + t, n_col)}, device_id_type=MESH)
    for t in range(1, n_row):
        pl.semaphore_signal(barrier, inc=1, device_id={"row": lax.rem(r + t, n_row)}, device_id_type=MESH)
    row_buf[zero] = jnp.zeros(row_buf.shape[1:], row_buf.dtype)
    acc[...] = jnp.zeros_like(acc)
    load_row.wait()
    load_col.wait()
    pl.semaphore_wait(barrier, n_col + n_row - 2)

    sends = []

    def send_row(cc, h, dest):
        copy = pltpu.make_async_remote_copy(
            src_ref=row_block(cc, h), dst_ref=row_block(cc, h),
            send_sem=row_send.at[len(sends)], recv_sem=row_recv.at[cc, h],
            device_id={"col": dest}, device_id_type=MESH)
        copy.start()
        sends.append(copy)

    def got_row(cc, h):
        pltpu.make_async_remote_copy(
            src_ref=row_block(cc, h), dst_ref=row_block(cc, h),
            send_sem=row_send.at[0], recv_sem=row_recv.at[cc, h],
            device_id={"col": lax.rem(c + 1, n_col)}, device_id_type=MESH).wait_recv()

    def col_copy(rr, way, dest):
        return pltpu.make_async_remote_copy(
            src_ref=col_block(rr), dst_ref=col_block(rr),
            send_sem=col_send.at[rr, way], recv_sem=col_recv.at[rr],
            device_id={"row": dest}, device_id_type=MESH)

    def other(value, t, n):
        return lax.rem(value + t, n)

    def pass_on(t):
        up, down = r - t, r + t
        if t > 0:
            @pl.when(up >= 0)
            def _():
                col_copy(up, 0, r).wait_recv()
        @pl.when((up >= 0) & (r < n_row - 1))
        def _():
            col_copy(up, 0, r + 1).start()
        if t > 0:
            @pl.when(down < n_row)
            def _():
                col_copy(down, 1, r).wait_recv()
        @pl.when((down < n_row) & (r > 0))
        def _():
            col_copy(down, 1, r - 1).start()

    pass_on(0)
    xs = [col_of(y, other(x, t, X), u) for t in range(1, X)]
    ys = [col_of(other(y, t, Y), x, u) for t in range(1, Y)]
    for dest in xs:
        send_row(c, 0, dest)
    for dest in ys:
        send_row(c, 1, dest)
    load_ri.wait()
    load_ci.wait()
    idx_copies = []
    for t in range(1, n_col):
        idx_copies.append(pltpu.make_async_remote_copy(
            src_ref=row_idx.at[c], dst_ref=row_idx.at[c],
            send_sem=idx_send.at[t - 1], recv_sem=idx_recv.at[t - 1],
            device_id={"col": other(c, t, n_col)}, device_id_type=MESH))
    for t in range(1, n_row):
        idx_copies.append(pltpu.make_async_remote_copy(
            src_ref=col_idx.at[r], dst_ref=col_idx.at[r],
            send_sem=idx_send.at[n_col - 2 + t], recv_sem=idx_recv.at[n_col - 2 + t],
            device_id={"row": other(r, t, n_row)}, device_id_type=MESH))
    for copy in idx_copies:
        copy.start()
    for dest in ys:
        send_row(c, 0, dest)
    for dest in xs:
        send_row(c, 1, dest)
    for h in range(2):
        send_row(c, h, c + 1 - 2 * u)
    for t in range(1, max(X, Y)):
        if t < X:
            cc = col_of(y, other(x, t, X), u)
            got_row(cc, 0)
            for dest in ys:
                send_row(cc, 0, dest)
        if t < Y:
            cc = col_of(other(y, t, Y), x, u)
            got_row(cc, 1)
            for dest in xs:
                send_row(cc, 1, dest)
    for t in range(1, X):
        send_row(col_of(y, other(x, t, X), u), 0, c + 1 - 2 * u)
    for t in range(1, Y):
        send_row(col_of(other(y, t, Y), x, u), 1, c + 1 - 2 * u)
    if n_row > 1:
        pass_on(1)
    for t in range(1, X):
        cc = col_of(y, other(x, t, X), u)
        got_row(cc, 1)
        send_row(cc, 1, c + 1 - 2 * u)
    for t in range(1, Y):
        cc = col_of(other(y, t, Y), x, u)
        got_row(cc, 0)
        send_row(cc, 0, c + 1 - 2 * u)
    for tx in range(1, X):
        for ty in range(1, Y):
            cc = col_of(other(y, ty, Y), other(x, tx, X), u)
            for h in range(2):
                got_row(cc, h)
                send_row(cc, h, c + 1 - 2 * u)
    for m in range(n_col // 2):
        for h in range(2):
            got_row(2 * m + 1 - u, h)
    for copy in idx_copies:
        copy.wait()
    to_smem = [pltpu.make_async_copy(row_idx, row_smem, smem_sem.at[0]),
               pltpu.make_async_copy(col_idx, col_smem, smem_sem.at[1])]
    for copy in to_smem:
        copy.start()
    for copy in to_smem:
        copy.wait()

    def unit(rr):
        def step(b, carry):
            middle = b * n_row + rr
            block = lax.rem(middle, n_col)
            left = []
            for a in range(rows):
                index = jnp.int32(zero)
                for s in range(slots):
                    index = jnp.where(row_smem[block, a, s] == middle, block * n_tiles + a * slots + s, index)
                left.append(row_buf[index])
            left = jnp.concatenate(left, axis=0)
            right = jnp.concatenate(
                [col_buf[rr * n_tiles + b * slots + s] for s in range(slots)], axis=1)
            paths = jnp.dot(left, right, preferred_element_type=jnp.float32)
            for a in range(rows):
                value = acc[a]
                for s in range(slots):
                    target = col_smem[rr, b, s]
                    index = jnp.int32(zero)
                    for q in range(slots):
                        own = row_smem[c, a, q]
                        index = jnp.where((own == target) & (target >= 0), c * n_tiles + a * slots + q, index)
                    value = value + paths[a * width:(a + 1) * width, s * width:(s + 1) * width] * (
                        row_buf[index].astype(jnp.float32))
                acc[a] = value
            return carry
        lax.fori_loop(0, rows, step, 0)

    def units(t):
        @pl.when(r - t >= 0)
        def _():
            unit(r - t)
        @pl.when(r + t < n_row)
        def _():
            unit(r + t)

    for t in range(2, n_row - 1):
        pass_on(t)
    unit(r)
    for t in range(1, n_row - 1):
        units(t)
    if n_row > 2:
        pass_on(n_row - 1)
    if n_row > 1:
        units(n_row - 1)

    parts[c] = jnp.sum(acc[...], axis=2)
    out_copies = []
    for t in range(1, n_col):
        out_copies.append(pltpu.make_async_remote_copy(
            src_ref=parts.at[c], dst_ref=parts.at[c],
            send_sem=part_send.at[t - 1], recv_sem=part_recv.at[t - 1],
            device_id={"col": other(c, t, n_col)}, device_id_type=MESH))
    for copy in out_copies:
        copy.start()
    for copy in sends:
        copy.wait_send()
    for t in range(n_row):
        @pl.when((r - t >= 0) & (r < n_row - 1))
        def _():
            col_copy(r - t, 0, r).wait_send()
        @pl.when((r + t < n_row) & (r > 0))
        def _():
            col_copy(r + t, 1, r).wait_send()
    for copy in out_copies:
        copy.wait()
    plane = jnp.sum(parts[...], axis=0)
    plane_ref[...] = plane
    planes[r] = plane
    plane_copies = []
    for t in range(1, n_row):
        plane_copies.append(pltpu.make_async_remote_copy(
            src_ref=planes.at[r], dst_ref=planes.at[r],
            send_sem=plane_send.at[t - 1], recv_sem=plane_recv.at[t - 1],
            device_id={"row": other(r, t, n_row)}, device_id_type=MESH))
    for copy in plane_copies:
        copy.start()
    for copy in plane_copies:
        copy.wait()
    total_ref[...] = jnp.full(total_ref.shape, jnp.sum(planes[...]), jnp.float32)


def on_device(n_row, n_col, tile_data, tile_cols):
    rows = tile_data.shape[0]
    slots = tile_data.shape[3]
    width = tile_data.shape[4]
    n_tiles = rows * slots
    tiles = tile_data.reshape(n_tiles, width, width)
    cols = jnp.pad(tile_cols.reshape(rows, slots), ((0, 0), (0, 128 - slots)), constant_values=-1)
    Y, X = plane_shape(n_col)
    n_sends = 2 * (n_col + (X - 1) + (Y - 1)) + (X - 1) * (Y - 1) * 2 + (X - 1) + (Y - 1) + 8
    dma = pltpu.SemaphoreType.DMA
    plane, total = pl.pallas_call(
        functools.partial(kernel, n_row, n_col),
        out_shape=(jax.ShapeDtypeStruct((rows, width), jnp.float32),
                   jax.ShapeDtypeStruct((8, 128), jnp.float32)),
        in_specs=[pl.BlockSpec(memory_space=pl.ANY), pl.BlockSpec(memory_space=pl.ANY)],
        out_specs=(pl.BlockSpec(memory_space=pltpu.VMEM), pl.BlockSpec(memory_space=pltpu.VMEM)),
        scratch_shapes=[
            pltpu.VMEM((n_col * n_tiles + 1, width, width), jnp.bfloat16),
            pltpu.VMEM((n_row * n_tiles, width, width), jnp.bfloat16),
            pltpu.VMEM((n_col, rows, 128), jnp.int32),
            pltpu.VMEM((n_row, rows, 128), jnp.int32),
            pltpu.SMEM((n_col, rows, 128), jnp.int32),
            pltpu.SMEM((n_row, rows, 128), jnp.int32),
            pltpu.VMEM((rows, width, width), jnp.float32),
            pltpu.VMEM((n_col, rows, width), jnp.float32),
            pltpu.VMEM((n_row, rows, width), jnp.float32),
            dma((4,)), dma((2,)),
            dma((n_sends,)), dma((n_col, 2)),
            dma((n_row, 2)), dma((n_row,)),
            dma((n_col + n_row - 2,)), dma((n_col + n_row - 2,)),
            dma((n_col - 1,)), dma((n_col - 1,)),
            dma((max(n_row - 1, 1),)), dma((max(n_row - 1, 1),)),
        ],
        compiler_params=pltpu.CompilerParams(collective_id=0, has_side_effects=True),
    )(tiles, cols)
    share = width // n_col
    start = lax.axis_index("col") * share
    shares = lax.dynamic_slice_in_dim(plane, start, share, 1).reshape(rows, 1, share)
    vertices = rows * n_row * width
    return shares * vertex_scale, total[0, 0] * (total_scale / vertices)


def solution(mesh):
    return jax.shard_map(
        functools.partial(on_device, mesh.shape["row"], mesh.shape["col"]),
        mesh=mesh,
        in_specs=(P(None, "row", "col", None, None, None), P(None, "row", "col", None)),
        out_specs=(P(None, "row", "col"), P()),
        check_vma=False,
    )
```

time: 215 us -> 58.8 us (0.27)
  waiting for transfers between devices: 63.6 us -> 0 us
  blocking collectives: 61 us -> 0 us
  Pallas kernels: 0 us -> 52.9 us
  local copies, waits for them, and re-layouts: 44.8 us -> 2.54 us
  matrix products: 26.4 us -> 0 us
  between operations: 15.6 us -> 2.45 us
    all_gather x2 -> x0, waiting for transfers between devices: 62.2 us -> none  [the longest x1 37.3 us: gathered(): return lax.all_gather(part, axis, axis=dim, tiled=True)]
    pallas_call x0 -> x1, Pallas kernels: none -> 52.9 us  [on_device(): pl.pallas_call(functools.partial(kernel, n_row, n_col), out_shape=(jax.Sh...]
    psum x1 -> x0, blocking collectives: 39.5 us -> none  [on_device(): overall = lax.psum(jnp.sum(partial_value), ('row', 'col'))]
    dot_general x16 -> x0, matrix products: 26.4 us -> none  [the longest x8 14.9 us: tile_counts(): jnp.einsum('pxy,pqyz->pqxz', stored, partner, preferred_element_type=jnp....]
    gather x24 -> x0, local copies, waits for them, and re-layouts: 25 us -> none  [the longest x8 19.9 us: tile_counts(): partner = col_tiles[clipped]]
    all_gather x2 -> x0, blocking collectives: 21.5 us -> none  [the longest x1 12.7 us: on_device(): col_index = lax.all_gather(tile_cols, 'row', axis=1, tiled=True)]
    dot_general x8 -> x0, local copies, waits for them, and re-layouts: 14.7 us -> none  [tile_counts(): jnp.einsum('pqs,sxz->pqxz', weights, own_tiles, preferred_element_type=jn...]
    unnamed x7 -> x4, local copies, waits for them, and re-layouts: 4.42 us -> 0.68 us
  transfers between devices with their start and end apart: 3 -> 0, of which waited for: 2 -> 0; matrix products, arithmetic and copies ran while one was open for 2% -> 0% of each run, Pallas kernels for 0% -> 0%
where the time goes in v1:
time: 58.8 us; the launch traced here: 58.6 us
  Pallas kernels  52.9 us (90%)
  local copies, waits for them, and re-layouts  2.54 us (4%)
  between operations  2.45 us (4%)
  other arithmetic  0.67 us (1%)
    pallas_call x1, Pallas kernels, on_device(): pl.pallas_call(functools.partial(kernel, n_row, n_col), out_shape=(jax.Sh...  52.9 us
    slice x1, local copies, waits for them, and re-layouts, on_device(): return (shares * vertex_scale, total[0, 0] * (total_scale / vertices))  1.19 us

profile of v1, /device:TPU:0, one launch (start us, length us, event | category | flops | bytes accessed | tf_op | source)
XLA Modules:
  0.0 58.6 jit_solution(11141496112330747122)
XLA Ops:
  0.6 0.0 copy-start.1
  0.6 0.7 %copy-done.1 = s32[8,1,1,2]{0,3,2,1:T(2,128)S(1)} copy-done((s32[8,1,1,2]{0,3,2,1:T(2,128)S(1)}, s32[8,1,1,2]{0,3,2,1:T(2,128)}, u32[]{:S(2)}) %copy-start.1) | copy-done | bytes 88
  1.3 0.1 copy.4
  1.4 0.6 %pad.4.cols_ref = s32[8,128]{1,0:T(8,128)} pad(s32[8,2]{1,0:T(8,128)S(1)} %copy.4, s32[]{:T(128)} %constant.7.clone.1), padding=0_0x0_126 | pad | bytes 4164 | tf_op jit(solution)/shard_map/jit(_pad)/pad | solution.py:269
  2.0 52.9 %shard_map.41 = (f32[8,128]{1,0:T(8,128)}, f32[8,128]{1,0:T(8,128)}) custom-call(bf16[16,128,128]{2,1,0:T(8,128)(2,1)} %bitcast.6, s32[8,128]{1,0:T(8,128)} %pad.4.cols_ref), custom_call_target="tpu_custom_call" | custom-call | tf_op jit(solution)/shard_map/pallas_call | solution.py:273
  54.9 0.0 copy-start
  54.9 1.2 %slice.3 = f32[1,1]{1,0:T(1,128)} slice(f32[8,128]{1,0:T(8,128)} %get-tuple-element.5), slice={[0:1], [0:1]} | slice | bytes 8 | tf_op jit(solution)/shard_map/slice | solution.py:302
  56.8 0.0 copy-done
  56.8 0.7 %dynamic-slice_multiply_fusion = f32[8,16]{1,0:T(8,128)} fusion(f32[8,128]{1,0:T(8,128)S(1)} %copy-done, s32[]{:T(128)S(6)} %select_n.3), kind=kLoop, calls=%fused_computation | loop fusion | flops 128 | bytes 1028 | tf_op jit(solution)/shard_map/mul | solution.py:302
Async XLA Ops:
  0.6 0.7 %copy-start.1 = (s32[8,1,1,2]{0,3,2,1:T(2,128)S(1)}, s32[8,1,1,2]{0,3,2,1:T(2,128)}, u32[]{:S(2)}) copy-start(s32[8,1,1,2]{0,3,2,1:T(2,128)} %param.3) | copy-start | bytes 196
  54.9 1.9 %copy-start = (f32[8,128]{1,0:T(8,128)S(1)}, f32[8,128]{1,0:T(8,128)}, u32[]{:S(2)}) copy-start(f32[8,128]{1,0:T(8,128)} %get-tuple-element.4) | copy-start | bytes 12292

commit v2 on v1

--- a/solution.py
+++ b/solution.py
@@ -20,9 +20,11 @@
 
 
 def kernel(n_row, n_col, tiles, cols_ref, plane_ref, total_ref,
-           row_buf, col_buf, row_idx, col_idx, row_smem, col_smem, acc, parts, planes,
+           row_buf, col_buf, far_buf, row_idx, col_idx, far_idx, row_smem, col_smem, far_smem,
+           acc, far_acc, parts, planes,
            load_sem, smem_sem, row_send, row_recv, col_send, col_recv,
-           idx_send, idx_recv, part_send, part_recv, plane_send, plane_recv):
+           idx_send, idx_recv, part_send, part_recv, plane_send, plane_recv,
+           far_send, far_recv, fidx_send, fidx_recv, fpart_send, fpart_recv):
     r = lax.axis_index("row")
     c = lax.axis_index("col")
     n_tiles = tiles.shape[0]
@@ -31,6 +33,16 @@
     slots = n_tiles // rows
     width = tiles.shape[1]
     zero = n_col * n_tiles
+    moved = n_row >= 4 and n_col % n_row == 0
+    reach = n_row - 2 if moved else n_row - 1
+    n_far = max(n_col // n_row, 1)
+    far_zero = n_far * n_tiles
+    low = r < n_row // 2
+    inner = (r == 1) | (r == n_row - 2)
+    outer = (r == 0) | (r == n_row - 1)
+    far_left = jnp.where(low, 0, n_row - 1)
+    far_middle = n_row - 1 - far_left
+    neighbour = jnp.where(low, 1 - r, 2 * n_row - 3 - r)
     Y, X = plane_shape(n_col)
     u = c % 2
     x = (c // 2) % X
@@ -59,11 +71,22 @@
         pl.semaphore_signal(barrier, inc=1, device_id={"col": lax.rem(c + t, n_col)}, device_id_type=MESH)
     for t in range(1, n_row):
         pl.semaphore_signal(barrier, inc=1, device_id={"row": lax.rem(r + t, n_row)}, device_id_type=MESH)
+    if moved:
+        @pl.when(inner | outer)
+        def _():
+            for t in range(1, n_col):
+                pl.semaphore_signal(
+                    barrier, inc=1, device_id={"row": neighbour, "col": lax.rem(c + t, n_col)},
+                    device_id_type=MESH)
     row_buf[zero] = jnp.zeros(row_buf.shape[1:], row_buf.dtype)
+    far_buf[far_zero] = jnp.zeros(far_buf.shape[1:], far_buf.dtype)
+    col_buf[n_row * n_tiles] = jnp.zeros(col_buf.shape[1:], col_buf.dtype)
     acc[...] = jnp.zeros_like(acc)
+    far_acc[...] = jnp.zeros_like(far_acc)
     load_row.wait()
     load_col.wait()
-    pl.semaphore_wait(barrier, n_col + n_row - 2)
+    greeted = jnp.where(inner | outer, n_col - 1, 0) if moved else 0
+    pl.semaphore_wait(barrier, n_col + n_row - 2 + greeted)
 
     sends = []
 
@@ -96,16 +119,18 @@
             @pl.when(up >= 0)
             def _():
                 col_copy(up, 0, r).wait_recv()
-        @pl.when((up >= 0) & (r < n_row - 1))
-        def _():
-            col_copy(up, 0, r + 1).start()
+        if t < reach:
+            @pl.when((up >= 0) & (r < n_row - 1))
+            def _():
+                col_copy(up, 0, r + 1).start()
         if t > 0:
             @pl.when(down < n_row)
             def _():
                 col_copy(down, 1, r).wait_recv()
-        @pl.when((down < n_row) & (r > 0))
-        def _():
-            col_copy(down, 1, r - 1).start()
+        if t < reach:
+            @pl.when((down < n_row) & (r > 0))
+            def _():
+                col_copy(down, 1, r - 1).start()
 
     pass_on(0)
     xs = [col_of(y, other(x, t, X), u) for t in range(1, X)]
@@ -152,6 +177,133 @@
         send_row(col_of(other(y, t, Y), x, u), 1, c + 1 - 2 * u)
     if n_row > 1:
         pass_on(1)
+
+    ways = X + Y
+
+    def far_block(e, h):
+        return far_buf.at[pl.ds(e * n_tiles + h * half, half)]
+
+    def far_copy(e, h, way, dest, source=None):
+        return pltpu.make_async_remote_copy(
+            src_ref=far_block(e, h) if source is None else source, dst_ref=far_block(e, h),
+            send_sem=far_send.at[e, h, way], recv_sem=far_recv.at[e, h],
+            device_id={"col": dest}, device_id_type=MESH)
+
+    def far_index(e, t):
+        return pltpu.make_async_remote_copy(
+            src_ref=far_idx.at[e], dst_ref=far_idx.at[e],
+            send_sem=fidx_send.at[e, t - 1], recv_sem=fidx_recv.at[e],
+            device_id={"col": other(c, t, n_col)}, device_id_type=MESH)
+
+    def far_tiles(e):
+        return pltpu.make_async_copy(
+            col_buf.at[pl.ds(far_left * n_tiles, n_tiles)],
+            far_buf.at[pl.ds(e * n_tiles, n_tiles)], load_sem.at[4])
+
+    def far_place(e):
+        cc = e * n_row + far_middle
+        return cc, (cc % 2) == u, ((cc // 2) % X) == x, (cc // (2 * X)) == y
+
+    partner = c + 1 - 2 * u
+    to_x = [(t, dest) for t, dest in enumerate(xs, 1)]
+    to_y = [(X - 1 + t, dest) for t, dest in enumerate(ys, 1)]
+
+    def far_source():
+        for e in range(n_far):
+            cc, same_u, same_x, same_y = far_place(e)
+
+            @pl.when(inner & (cc == c))
+            def _():
+                source = col_buf.at[pl.ds(far_left * n_tiles, half)]
+                source2 = col_buf.at[pl.ds(far_left * n_tiles + half, half)]
+                for way, dest in to_x:
+                    far_copy(e, 0, way, dest, source).start()
+                for way, dest in to_y:
+                    far_copy(e, 1, way, dest, source2).start()
+                for way, dest in to_y:
+                    far_copy(e, 0, way, dest, source).start()
+                for way, dest in to_x:
+                    far_copy(e, 1, way, dest, source2).start()
+                far_copy(e, 0, 0, partner, source).start()
+                far_copy(e, 1, 0, partner, source2).start()
+                far_tiles(e).start()
+                index = pltpu.make_async_copy(col_idx.at[far_left], far_idx.at[e], load_sem.at[5])
+                index.start()
+                index.wait()
+                for t in range(1, n_col):
+                    far_index(e, t).start()
+
+    def far_relay(first):
+        for e in range(n_far):
+            cc, same_u, same_x, same_y = far_place(e)
+            here = inner & same_u & (cc != c)
+
+            @pl.when(here & same_y)
+            def _():
+                h = 0 if first else 1
+                far_copy(e, h, 0, partner).wait_recv()
+                if first:
+                    for way, dest in to_y:
+                        far_copy(e, 0, way, dest).start()
+                far_copy(e, h, 0, partner).start()
+
+            @pl.when(here & same_x)
+            def _():
+                h = 1 if first else 0
+                far_copy(e, h, 0, partner).wait_recv()
+                if first:
+                    for way, dest in to_x:
+                        far_copy(e, 1, way, dest).start()
+                far_copy(e, h, 0, partner).start()
+
+            if not first:
+                @pl.when(here & jnp.logical_not(same_x | same_y))
+                def _():
+                    for h in range(2):
+                        far_copy(e, h, 0, partner).wait_recv()
+                        far_copy(e, h, 0, partner).start()
+
+    def far_end():
+        for e in range(n_far):
+            cc, same_u, same_x, same_y = far_place(e)
+
+            @pl.when(inner & jnp.logical_not(same_u))
+            def _():
+                for h in range(2):
+                    far_copy(e, h, 0, partner).wait_recv()
+
+            @pl.when(inner & (cc != c))
+            def _():
+                far_index(e, 1).wait_recv()
+
+            @pl.when(inner & (cc == c))
+            def _():
+                far_tiles(e).wait()
+                for t in range(1, n_col):
+                    far_index(e, t).wait_send()
+                for h in range(2):
+                    for way in range(ways - 1):
+                        far_copy(e, h, way, partner).wait_send()
+
+            @pl.when(inner & same_u & (cc != c))
+            def _():
+                for h in range(2):
+                    far_copy(e, h, 0, partner).wait_send()
+
+            @pl.when(inner & same_u & (cc != c) & same_y)
+            def _():
+                for way, dest in to_y:
+                    far_copy(e, 0, way, dest).wait_send()
+
+            @pl.when(inner & same_u & (cc != c) & same_x)
+            def _():
+                for way, dest in to_x:
+                    far_copy(e, 1, way, dest).wait_send()
+
+    for copy in idx_copies:
+        copy.wait()
+    if moved:
+        far_source()
     for t in range(1, X):
         cc = col_of(y, other(x, t, X), u)
         got_row(cc, 1)
@@ -169,8 +321,6 @@
     for m in range(n_col // 2):
         for h in range(2):
             got_row(2 * m + 1 - u, h)
-    for copy in idx_copies:
-        copy.wait()
     to_smem = [pltpu.make_async_copy(row_idx, row_smem, smem_sem.at[0]),
                pltpu.make_async_copy(col_idx, col_smem, smem_sem.at[1])]
     for copy in to_smem:
@@ -178,51 +328,89 @@
     for copy in to_smem:
         copy.wait()
 
-    def unit(rr):
+    def unit(rr, left_slot, left_buf, left_zero, own_slot, own_buf, own_zero, own_base, total):
         def step(b, carry):
             middle = b * n_row + rr
             block = lax.rem(middle, n_col)
             left = []
             for a in range(rows):
-                index = jnp.int32(zero)
+                index = jnp.int32(left_zero)
                 for s in range(slots):
-                    index = jnp.where(row_smem[block, a, s] == middle, block * n_tiles + a * slots + s, index)
-                left.append(row_buf[index])
+                    held, base = left_slot(block, a, s)
+                    index = jnp.where(held == middle, base + a * slots + s, index)
+                left.append(left_buf[index])
             left = jnp.concatenate(left, axis=0)
             right = jnp.concatenate(
                 [col_buf[rr * n_tiles + b * slots + s] for s in range(slots)], axis=1)
             paths = jnp.dot(left, right, preferred_element_type=jnp.float32)
             for a in range(rows):
-                value = acc[a]
+                value = total[a]
                 for s in range(slots):
                     target = col_smem[rr, b, s]
-                    index = jnp.int32(zero)
+                    index = jnp.int32(own_zero)
                     for q in range(slots):
-                        own = row_smem[c, a, q]
-                        index = jnp.where((own == target) & (target >= 0), c * n_tiles + a * slots + q, index)
+                        own = own_slot(a, q)
+                        index = jnp.where((own == target) & (target >= 0), own_base + a * slots + q, index)
                     value = value + paths[a * width:(a + 1) * width, s * width:(s + 1) * width] * (
-                        row_buf[index].astype(jnp.float32))
-                acc[a] = value
+                        own_buf[index].astype(jnp.float32))
+                total[a] = value
             return carry
         lax.fori_loop(0, rows, step, 0)
 
+    def near_unit(rr):
+        unit(rr, lambda block, a, s: (row_smem[block, a, s], block * n_tiles), row_buf, zero,
+             lambda a, q: row_smem[c, a, q], row_buf, zero, c * n_tiles, acc)
+
+    def far_unit():
+        unit(far_middle,
+             lambda block, a, s: (far_smem[block // n_row, a, s], (block // n_row) * n_tiles),
+             far_buf, far_zero,
+             lambda a, q: col_smem[far_left, a, q], col_buf, n_row * n_tiles,
+             far_left * n_tiles, far_acc)
+
     def units(t):
         @pl.when(r - t >= 0)
         def _():
-            unit(r - t)
+            near_unit(r - t)
         @pl.when(r + t < n_row)
         def _():
-            unit(r + t)
-
-    for t in range(2, n_row - 1):
+            near_unit(r + t)
+
+    for t in range(2, reach):
         pass_on(t)
-    unit(r)
-    for t in range(1, n_row - 1):
+    if moved:
+        far_relay(True)
+    near_unit(r)
+    for t in range(1, reach):
         units(t)
-    if n_row > 2:
-        pass_on(n_row - 1)
-    if n_row > 1:
-        units(n_row - 1)
+    if moved:
+        far_relay(False)
+    if reach > 1:
+        pass_on(reach)
+    if reach > 0:
+        units(reach)
+    if moved:
+        far_end()
+
+        @pl.when(inner)
+        def _():
+            copy = pltpu.make_async_copy(far_idx, far_smem, smem_sem.at[2])
+            copy.start()
+            copy.wait()
+            far_unit()
+            parts[n_col + c] = jnp.sum(far_acc[...], axis=2)
+
+    def far_part(t):
+        return pltpu.make_async_remote_copy(
+            src_ref=parts.at[n_col + c], dst_ref=parts.at[n_col + c],
+            send_sem=fpart_send.at[t], recv_sem=fpart_recv.at[t],
+            device_id={"row": neighbour, "col": other(c, t, n_col)}, device_id_type=MESH)
+
+    if moved:
+        @pl.when(inner)
+        def _():
+            for t in range(n_col):
+                far_part(t).start()
 
     parts[c] = jnp.sum(acc[...], axis=2)
     out_copies = []
@@ -235,7 +423,7 @@
         copy.start()
     for copy in sends:
         copy.wait_send()
-    for t in range(n_row):
+    for t in range(reach):
         @pl.when((r - t >= 0) & (r < n_row - 1))
         def _():
             col_copy(r - t, 0, r).wait_send()
@@ -244,9 +432,19 @@
             col_copy(r + t, 1, r).wait_send()
     for copy in out_copies:
         copy.wait()
-    plane = jnp.sum(parts[...], axis=0)
-    plane_ref[...] = plane
-    planes[r] = plane
+    planes[r] = jnp.sum(parts[0:n_col], axis=0)
+    if moved:
+        @pl.when(inner)
+        def _():
+            for t in range(n_col):
+                far_part(t).wait_send()
+
+        @pl.when(outer)
+        def _():
+            for t in range(n_col):
+                far_part(t).wait_recv()
+            planes[r] = planes[r] + jnp.sum(parts[n_col:2 * n_col], axis=0)
+    plane_ref[...] = planes[r]
     plane_copies = []
     for t in range(1, n_row):
         plane_copies.append(pltpu.make_async_remote_copy(
@@ -268,6 +466,7 @@
     tiles = tile_data.reshape(n_tiles, width, width)
     cols = jnp.pad(tile_cols.reshape(rows, slots), ((0, 0), (0, 128 - slots)), constant_values=-1)
     Y, X = plane_shape(n_col)
+    n_far = max(n_col // n_row, 1)
     n_sends = 2 * (n_col + (X - 1) + (Y - 1)) + (X - 1) * (Y - 1) * 2 + (X - 1) + (Y - 1) + 8
     dma = pltpu.SemaphoreType.DMA
     plane, total = pl.pallas_call(
@@ -278,20 +477,27 @@
         out_specs=(pl.BlockSpec(memory_space=pltpu.VMEM), pl.BlockSpec(memory_space=pltpu.VMEM)),
         scratch_shapes=[
             pltpu.VMEM((n_col * n_tiles + 1, width, width), jnp.bfloat16),
-            pltpu.VMEM((n_row * n_tiles, width, width), jnp.bfloat16),
+            pltpu.VMEM((n_row * n_tiles + 1, width, width), jnp.bfloat16),
+            pltpu.VMEM((n_far * n_tiles + 1, width, width), jnp.bfloat16),
             pltpu.VMEM((n_col, rows, 128), jnp.int32),
             pltpu.VMEM((n_row, rows, 128), jnp.int32),
+            pltpu.VMEM((n_far, rows, 128), jnp.int32),
             pltpu.SMEM((n_col, rows, 128), jnp.int32),
             pltpu.SMEM((n_row, rows, 128), jnp.int32),
+            pltpu.SMEM((n_far, rows, 128), jnp.int32),
             pltpu.VMEM((rows, width, width), jnp.float32),
-            pltpu.VMEM((n_col, rows, width), jnp.float32),
+            pltpu.VMEM((rows, width, width), jnp.float32),
+            pltpu.VMEM((2 * n_col, rows, width), jnp.float32),
             pltpu.VMEM((n_row, rows, width), jnp.float32),
-            dma((4,)), dma((2,)),
+            dma((6,)), dma((3,)),
             dma((n_sends,)), dma((n_col, 2)),
             dma((n_row, 2)), dma((n_row,)),
             dma((n_col + n_row - 2,)), dma((n_col + n_row - 2,)),
             dma((n_col - 1,)), dma((n_col - 1,)),
             dma((max(n_row - 1, 1),)), dma((max(n_row - 1, 1),)),
+            dma((n_far, 2, X + Y)), dma((n_far, 2)),
+            dma((n_far, n_col - 1)), dma((n_far,)),
+            dma((n_col,)), dma((n_col,)),
         ],
         compiler_params=pltpu.CompilerParams(collective_id=0, has_side_effects=True),
     )(tiles, cols)

time: 58.8 us -> 55.4 us (0.942)
  Pallas kernels: 52.9 us -> 49.5 us
    pallas_call x1, Pallas kernels: 52.9 us -> 49.5 us  [on_device(): pl.pallas_call(functools.partial(kernel, n_row, n_col), out_shape=(jax.Sh...]
where the time goes in v2:
time: 55.4 us; the launch traced here: 55.2 us
  Pallas kernels  49.5 us (89%)
  local copies, waits for them, and re-layouts  2.54 us (5%)
  between operations  2.45 us (4%)
  other arithmetic  0.67 us (1%)
    pallas_call x1, Pallas kernels, on_device(): pl.pallas_call(functools.partial(kernel, n_row, n_col), out_shape=(jax.Sh...  49.5 us
    slice x1, local copies, waits for them, and re-layouts, on_device(): return (shares * vertex_scale, total[0, 0] * (total_scale / vertices))  1.19 us

profile of v2, /device:TPU:0, one launch (start us, length us, event | category | flops | bytes accessed | tf_op | source)
XLA Modules:
  0.0 55.2 jit_solution(7240972678875360923)
XLA Ops:
  0.6 0.0 copy-start.1
  0.6 0.7 %copy-done.1 = s32[8,1,1,2]{0,3,2,1:T(2,128)S(1)} copy-done((s32[8,1,1,2]{0,3,2,1:T(2,128)S(1)}, s32[8,1,1,2]{0,3,2,1:T(2,128)}, u32[]{:S(2)}) %copy-start.1) | copy-done | bytes 88
  1.3 0.1 copy.4
  1.4 0.6 %pad.4.cols_ref = s32[8,128]{1,0:T(8,128)} pad(s32[8,2]{1,0:T(8,128)S(1)} %copy.4, s32[]{:T(128)} %constant.7.clone.1), padding=0_0x0_126 | pad | bytes 4164 | tf_op jit(solution)/shard_map/jit(_pad)/pad | solution.py:467
  2.0 49.5 %shard_map.41 = (f32[8,128]{1,0:T(8,128)}, f32[8,128]{1,0:T(8,128)}) custom-call(bf16[16,128,128]{2,1,0:T(8,128)(2,1)} %bitcast.6, s32[8,128]{1,0:T(8,128)} %pad.4.cols_ref), custom_call_target="tpu_custom_call" | custom-call | tf_op jit(solution)/shard_map/pallas_call | solution.py:472
  51.5 0.0 copy-start
  51.5 1.2 %slice.3 = f32[1,1]{1,0:T(1,128)} slice(f32[8,128]{1,0:T(8,128)} %get-tuple-element.5), slice={[0:1], [0:1]} | slice | bytes 8 | tf_op jit(solution)/shard_map/slice | solution.py:508
  53.4 0.0 copy-done
  53.4 0.7 %dynamic-slice_multiply_fusion = f32[8,16]{1,0:T(8,128)} fusion(f32[8,128]{1,0:T(8,128)S(1)} %copy-done, s32[]{:T(128)S(6)} %select_n.3), kind=kLoop, calls=%fused_computation | loop fusion | flops 128 | bytes 1028 | tf_op jit(solution)/shard_map/mul | solution.py:508
Async XLA Ops:
  0.6 0.7 %copy-start.1 = (s32[8,1,1,2]{0,3,2,1:T(2,128)S(1)}, s32[8,1,1,2]{0,3,2,1:T(2,128)}, u32[]{:S(2)}) copy-start(s32[8,1,1,2]{0,3,2,1:T(2,128)} %param.3) | copy-start | bytes 196
  51.5 1.9 %copy-start = (f32[8,128]{1,0:T(8,128)S(1)}, f32[8,128]{1,0:T(8,128)}, u32[]{:S(2)}) copy-start(f32[8,128]{1,0:T(8,128)} %get-tuple-element.4) | copy-start | bytes 12292

commit v3 on v2

--- a/solution.py
+++ b/solution.py
@@ -19,11 +19,11 @@
     return (side, side) if side * side == chips else (1, chips)
 
 
-def kernel(n_row, n_col, tiles, cols_ref, plane_ref, total_ref,
+def kernel(n_row, n_col, tiles, cols_ref, share_ref, total_ref,
            row_buf, col_buf, far_buf, row_idx, col_idx, far_idx, row_smem, col_smem, far_smem,
-           acc, far_acc, parts, planes,
+           acc, far_acc, parts, sums,
            load_sem, smem_sem, row_send, row_recv, col_send, col_recv,
-           idx_send, idx_recv, part_send, part_recv, plane_send, plane_recv,
+           idx_send, idx_recv, part_send, part_recv, sum_send, sum_recv,
            far_send, far_recv, fidx_send, fidx_recv, fpart_send, fpart_recv):
     r = lax.axis_index("row")
     c = lax.axis_index("col")
@@ -71,13 +71,6 @@
         pl.semaphore_signal(barrier, inc=1, device_id={"col": lax.rem(c + t, n_col)}, device_id_type=MESH)
     for t in range(1, n_row):
         pl.semaphore_signal(barrier, inc=1, device_id={"row": lax.rem(r + t, n_row)}, device_id_type=MESH)
-    if moved:
-        @pl.when(inner | outer)
-        def _():
-            for t in range(1, n_col):
-                pl.semaphore_signal(
-                    barrier, inc=1, device_id={"row": neighbour, "col": lax.rem(c + t, n_col)},
-                    device_id_type=MESH)
     row_buf[zero] = jnp.zeros(row_buf.shape[1:], row_buf.dtype)
     far_buf[far_zero] = jnp.zeros(far_buf.shape[1:], far_buf.dtype)
     col_buf[n_row * n_tiles] = jnp.zeros(col_buf.shape[1:], col_buf.dtype)
@@ -85,8 +78,7 @@
     far_acc[...] = jnp.zeros_like(far_acc)
     load_row.wait()
     load_col.wait()
-    greeted = jnp.where(inner | outer, n_col - 1, 0) if moved else 0
-    pl.semaphore_wait(barrier, n_col + n_row - 2 + greeted)
+    pl.semaphore_wait(barrier, n_col + n_row - 2)
 
     sends = []
 
@@ -346,7 +338,7 @@
             for a in range(rows):
                 value = total[a]
                 for s in range(slots):
-                    target = col_smem[rr, b, s]
+                    target = col_smem[rr, s, b]
                     index = jnp.int32(own_zero)
                     for q in range(slots):
                         own = own_slot(a, q)
@@ -358,14 +350,14 @@
         lax.fori_loop(0, rows, step, 0)
 
     def near_unit(rr):
-        unit(rr, lambda block, a, s: (row_smem[block, a, s], block * n_tiles), row_buf, zero,
-             lambda a, q: row_smem[c, a, q], row_buf, zero, c * n_tiles, acc)
+        unit(rr, lambda block, a, s: (row_smem[block, s, a], block * n_tiles), row_buf, zero,
+             lambda a, q: row_smem[c, q, a], row_buf, zero, c * n_tiles, acc)
 
     def far_unit():
         unit(far_middle,
-             lambda block, a, s: (far_smem[block // n_row, a, s], (block // n_row) * n_tiles),
+             lambda block, a, s: (far_smem[block // n_row, s, a], (block // n_row) * n_tiles),
              far_buf, far_zero,
-             lambda a, q: col_smem[far_left, a, q], col_buf, n_row * n_tiles,
+             lambda a, q: col_smem[far_left, q, a], col_buf, n_row * n_tiles,
              far_left * n_tiles, far_acc)
 
     def units(t):
@@ -398,7 +390,6 @@
             copy.start()
             copy.wait()
             far_unit()
-            parts[n_col + c] = jnp.sum(far_acc[...], axis=2)
 
     def far_part(t):
         return pltpu.make_async_remote_copy(
@@ -406,13 +397,29 @@
             send_sem=fpart_send.at[t], recv_sem=fpart_recv.at[t],
             device_id={"row": neighbour, "col": other(c, t, n_col)}, device_id_type=MESH)
 
-    if moved:
+    n_all = n_row * n_col
+    me = r * n_col + c
+    counts = jnp.sum(acc[...], axis=2)
+    parts[c] = counts
+    if moved:
+        far_counts = jnp.sum(far_acc[...], axis=2)
+
         @pl.when(inner)
         def _():
-            for t in range(n_col):
-                far_part(t).start()
-
-    parts[c] = jnp.sum(acc[...], axis=2)
+            parts[n_col + c] = far_counts
+
+        counts = counts + far_counts
+    sums[me] = jnp.sum(counts, axis=0, keepdims=True)
+
+    def send_sum(t, carry):
+        dest = lax.rem(me + t, n_all)
+        pltpu.make_async_remote_copy(
+            src_ref=sums.at[me], dst_ref=sums.at[me],
+            send_sem=sum_send.at[0], recv_sem=sum_recv.at[0],
+            device_id={"row": dest // n_col, "col": lax.rem(dest, n_col)}, device_id_type=MESH).start()
+        return carry
+
+    lax.fori_loop(1, n_all, send_sum, 0)
     out_copies = []
     for t in range(1, n_col):
         out_copies.append(pltpu.make_async_remote_copy(
@@ -421,6 +428,11 @@
             device_id={"col": other(c, t, n_col)}, device_id_type=MESH))
     for copy in out_copies:
         copy.start()
+    if moved:
+        @pl.when(inner)
+        def _():
+            for t in range(n_col):
+                far_part(t).start()
     for copy in sends:
         copy.wait_send()
     for t in range(reach):
@@ -432,30 +444,35 @@
             col_copy(r + t, 1, r).wait_send()
     for copy in out_copies:
         copy.wait()
-    planes[r] = jnp.sum(parts[0:n_col], axis=0)
     if moved:
         @pl.when(inner)
         def _():
             for t in range(n_col):
                 far_part(t).wait_send()
+            parts[n_col] = jnp.zeros(parts.shape[1:], parts.dtype)
 
         @pl.when(outer)
         def _():
             for t in range(n_col):
                 far_part(t).wait_recv()
-            planes[r] = planes[r] + jnp.sum(parts[n_col:2 * n_col], axis=0)
-    plane_ref[...] = planes[r]
-    plane_copies = []
-    for t in range(1, n_row):
-        plane_copies.append(pltpu.make_async_remote_copy(
-            src_ref=planes.at[r], dst_ref=planes.at[r],
-            send_sem=plane_send.at[t - 1], recv_sem=plane_recv.at[t - 1],
-            device_id={"row": other(r, t, n_row)}, device_id_type=MESH))
-    for copy in plane_copies:
-        copy.start()
-    for copy in plane_copies:
-        copy.wait()
-    total_ref[...] = jnp.full(total_ref.shape, jnp.sum(planes[...]), jnp.float32)
+            parts[n_col] = jnp.sum(parts[n_col:2 * n_col], axis=0)
+    plane = jnp.sum(parts[0:n_col], axis=0)
+    if moved:
+        @pl.when(jnp.logical_not(inner | outer))
+        def _():
+            parts[n_col] = jnp.zeros(parts.shape[1:], parts.dtype)
+        plane = plane + parts[n_col]
+    share = width // n_col
+    mine = pltpu.roll(plane, lax.rem(width - c * share, width), 1)
+    for a in range(rows):
+        share_ref[a] = mine[a:a + 1, 0:share] * vertex_scale
+    everyone = pltpu.make_async_remote_copy(
+        src_ref=sums.at[pl.ds(0, n_all - 1)], dst_ref=sums.at[pl.ds(0, n_all - 1)],
+        send_sem=sum_send.at[0], recv_sem=sum_recv.at[0],
+        device_id={"col": lax.rem(c + 1, n_col)}, device_id_type=MESH)
+    everyone.wait_send()
+    everyone.wait_recv()
+    total_ref[0, 0] = jnp.sum(sums[...]) * (total_scale / (rows * n_row * width))
 
 
 def on_device(n_row, n_col, tile_data, tile_cols):
@@ -464,48 +481,45 @@
     width = tile_data.shape[4]
     n_tiles = rows * slots
     tiles = tile_data.reshape(n_tiles, width, width)
-    cols = jnp.pad(tile_cols.reshape(rows, slots), ((0, 0), (0, 128 - slots)), constant_values=-1)
+    cols = jnp.transpose(tile_cols.reshape(rows, slots))
     Y, X = plane_shape(n_col)
     n_far = max(n_col // n_row, 1)
     n_sends = 2 * (n_col + (X - 1) + (Y - 1)) + (X - 1) * (Y - 1) * 2 + (X - 1) + (Y - 1) + 8
     dma = pltpu.SemaphoreType.DMA
-    plane, total = pl.pallas_call(
+    share = width // n_col
+    shares, total = pl.pallas_call(
         functools.partial(kernel, n_row, n_col),
-        out_shape=(jax.ShapeDtypeStruct((rows, width), jnp.float32),
-                   jax.ShapeDtypeStruct((8, 128), jnp.float32)),
+        out_shape=(jax.ShapeDtypeStruct((rows, 1, share), jnp.float32),
+                   jax.ShapeDtypeStruct((1, 1), jnp.float32)),
         in_specs=[pl.BlockSpec(memory_space=pl.ANY), pl.BlockSpec(memory_space=pl.ANY)],
-        out_specs=(pl.BlockSpec(memory_space=pltpu.VMEM), pl.BlockSpec(memory_space=pltpu.VMEM)),
+        out_specs=(pl.BlockSpec(memory_space=pltpu.VMEM), pl.BlockSpec(memory_space=pltpu.SMEM)),
         scratch_shapes=[
             pltpu.VMEM((n_col * n_tiles + 1, width, width), jnp.bfloat16),
             pltpu.VMEM((n_row * n_tiles + 1, width, width), jnp.bfloat16),
             pltpu.VMEM((n_far * n_tiles + 1, width, width), jnp.bfloat16),
-            pltpu.VMEM((n_col, rows, 128), jnp.int32),
-            pltpu.VMEM((n_row, rows, 128), jnp.int32),
-            pltpu.VMEM((n_far, rows, 128), jnp.int32),
-            pltpu.SMEM((n_col, rows, 128), jnp.int32),
-            pltpu.SMEM((n_row, rows, 128), jnp.int32),
-            pltpu.SMEM((n_far, rows, 128), jnp.int32),
+            pltpu.VMEM((n_col, slots, rows), jnp.int32),
+            pltpu.VMEM((n_row, slots, rows), jnp.int32),
+            pltpu.VMEM((n_far, slots, rows), jnp.int32),
+            pltpu.SMEM((n_col, slots, rows), jnp.int32),
+            pltpu.SMEM((n_row, slots, rows), jnp.int32),
+            pltpu.SMEM((n_far, slots, rows), jnp.int32),
             pltpu.VMEM((rows, width, width), jnp.float32),
             pltpu.VMEM((rows, width, width), jnp.float32),
             pltpu.VMEM((2 * n_col, rows, width), jnp.float32),
-            pltpu.VMEM((n_row, rows, width), jnp.float32),
+            pltpu.VMEM((n_row * n_col, 1, width), jnp.float32),
             dma((6,)), dma((3,)),
             dma((n_sends,)), dma((n_col, 2)),
             dma((n_row, 2)), dma((n_row,)),
             dma((n_col + n_row - 2,)), dma((n_col + n_row - 2,)),
             dma((n_col - 1,)), dma((n_col - 1,)),
-            dma((max(n_row - 1, 1),)), dma((max(n_row - 1, 1),)),
+            dma((1,)), dma((1,)),
             dma((n_far, 2, X + Y)), dma((n_far, 2)),
             dma((n_far, n_col - 1)), dma((n_far,)),
             dma((n_col,)), dma((n_col,)),
         ],
         compiler_params=pltpu.CompilerParams(collective_id=0, has_side_effects=True),
     )(tiles, cols)
-    share = width // n_col
-    start = lax.axis_index("col") * share
-    shares = lax.dynamic_slice_in_dim(plane, start, share, 1).reshape(rows, 1, share)
-    vertices = rows * n_row * width
-    return shares * vertex_scale, total[0, 0] * (total_scale / vertices)
+    return shares, total[0, 0]
 
 
 def solution(mesh):

time: 55.4 us -> 49.6 us (0.90)
  Pallas kernels: 49.5 us -> 45.8 us
  local copies, waits for them, and re-layouts: 2.54 us -> 1.26 us
  other arithmetic: 0.67 us -> 0 us
    pallas_call x1, Pallas kernels: 49.5 us -> 45.8 us  [on_device(): pl.pallas_call(functools.partial(kernel, n_row, n_col), out_shape=(jax.Sh...]
    slice x1 -> x0, local copies, waits for them, and re-layouts: 1.19 us -> none  [on_device(): return (shares * vertex_scale, total[0, 0] * (total_scale / vertices))]
    mul x1 -> x0, other arithmetic: 0.67 us -> none  [on_device(): return (shares * vertex_scale, total[0, 0] * (total_scale / vertices))]
    pad x1 -> x0, local copies, waits for them, and re-layouts: 0.6 us -> none  [on_device(): jnp.pad(tile_cols.reshape(rows, slots), ((0, 0), (0, 128 - slots)), const...]
    unnamed x4 -> x3, local copies, waits for them, and re-layouts: 0.68 us -> 1.26 us
where the time goes in v3:
time: 49.6 us; the launch traced here: 49.4 us
  Pallas kernels  45.8 us (92%)
  between operations  2.41 us (5%)
  local copies, waits for them, and re-layouts  1.26 us (3%)
    pallas_call x1, Pallas kernels, on_device(): pl.pallas_call(functools.partial(kernel, n_row, n_col), out_shape=(jax.Sh...  45.8 us
    unnamed x3, local copies, waits for them, and re-layouts  1.26 us

profile of v3, /device:TPU:0, one launch (start us, length us, event | category | flops | bytes accessed | tf_op | source)
XLA Modules:
  0.0 49.4 jit_solution(3037931651977743218)
XLA Ops:
  0.6 45.8 %shard_map.41 = (f32[8,1,16]{2,1,0:T(1,128)}, f32[1,1]{1,0:T(1,128)}) custom-call(bf16[16,128,128]{2,1,0:T(8,128)(2,1)} %bitcast.5, s32[2,8]{1,0:T(2,128)} %bitcast.6), custom_call_target="tpu_custom_call" | custom-call | tf_op jit(solution)/shard_map/pallas_call | solution.py:490
  46.4 0.0 copy-start
  46.4 0.7 %copy-done = f32[8,1,16]{2,1,0:T(1,128)S(1)} copy-done((f32[8,1,16]{2,1,0:T(1,128)S(1)}, f32[8,1,16]{2,1,0:T(1,128)}, u32[]{:S(2)}) %copy-start) | copy-done | bytes 536
  47.1 0.6 %copy.6 = f32[8,1,16]{2,1,0:T(1,128)} copy(f32[8,1,16]{2,1,0:T(1,128)S(1)} %copy-done) | data formatting | bytes 1024
Async XLA Ops:
  46.4 0.7 %copy-start = (f32[8,1,16]{2,1,0:T(1,128)S(1)}, f32[8,1,16]{2,1,0:T(1,128)}, u32[]{:S(2)}) copy-start(f32[8,1,16]{2,1,0:T(1,128)} %get-tuple-element.8) | copy-start | bytes 1540

commit v4 on v3

--- a/solution.py
+++ b/solution.py
@@ -264,10 +264,6 @@
                 for h in range(2):
                     far_copy(e, h, 0, partner).wait_recv()
 
-            @pl.when(inner & (cc != c))
-            def _():
-                far_index(e, 1).wait_recv()
-
             @pl.when(inner & (cc == c))
             def _():
                 far_tiles(e).wait()
@@ -294,6 +290,10 @@
 
     for copy in idx_copies:
         copy.wait()
+    to_smem = [pltpu.make_async_copy(row_idx, row_smem, smem_sem.at[0]),
+               pltpu.make_async_copy(col_idx, col_smem, smem_sem.at[1])]
+    for copy in to_smem:
+        copy.start()
     if moved:
         far_source()
     for t in range(1, X):
@@ -313,10 +313,6 @@
     for m in range(n_col // 2):
         for h in range(2):
             got_row(2 * m + 1 - u, h)
-    to_smem = [pltpu.make_async_copy(row_idx, row_smem, smem_sem.at[0]),
-               pltpu.make_async_copy(col_idx, col_smem, smem_sem.at[1])]
-    for copy in to_smem:
-        copy.start()
     for copy in to_smem:
         copy.wait()
 
@@ -331,21 +327,24 @@
                     held, base = left_slot(block, a, s)
                     index = jnp.where(held == middle, base + a * slots + s, index)
                 left.append(left_buf[index])
-            left = jnp.concatenate(left, axis=0)
             right = jnp.concatenate(
                 [col_buf[rr * n_tiles + b * slots + s] for s in range(slots)], axis=1)
-            paths = jnp.dot(left, right, preferred_element_type=jnp.float32)
+            own_rows = []
             for a in range(rows):
-                value = total[a]
+                pair = []
                 for s in range(slots):
                     target = col_smem[rr, s, b]
                     index = jnp.int32(own_zero)
                     for q in range(slots):
                         own = own_slot(a, q)
                         index = jnp.where((own == target) & (target >= 0), own_base + a * slots + q, index)
-                    value = value + paths[a * width:(a + 1) * width, s * width:(s + 1) * width] * (
-                        own_buf[index].astype(jnp.float32))
-                total[a] = value
+                    pair.append(own_buf[index])
+                own_rows.append(jnp.concatenate(pair, axis=1))
+            common = lax.dot_general(
+                jnp.concatenate(own_rows, axis=0), right, (((1,), (1,)), ((), ())),
+                preferred_element_type=jnp.float32)
+            for a in range(rows):
+                total[a] += common[a * width:(a + 1) * width] * left[a].astype(jnp.float32)
             return carry
         lax.fori_loop(0, rows, step, 0)
 
@@ -375,8 +374,17 @@
     near_unit(r)
     for t in range(1, reach):
         units(t)
+    far_to_smem = pltpu.make_async_copy(far_idx, far_smem, smem_sem.at[2])
     if moved:
         far_relay(False)
+        for e in range(n_far):
+            @pl.when(inner & (far_place(e)[0] != c))
+            def _():
+                far_index(e, 1).wait_recv()
+
+        @pl.when(inner)
+        def _():
+            far_to_smem.start()
     if reach > 1:
         pass_on(reach)
     if reach > 0:
@@ -386,9 +394,7 @@
 
         @pl.when(inner)
         def _():
-            copy = pltpu.make_async_copy(far_idx, far_smem, smem_sem.at[2])
-            copy.start()
-            copy.wait()
+            far_to_smem.wait()
             far_unit()
 
     def far_part(t):

time: 49.6 us -> 49 us (0.988)
  Pallas kernels: 45.8 us -> 45.2 us
    pallas_call x1, Pallas kernels: 45.8 us -> 45.2 us  [on_device(): pl.pallas_call(functools.partial(kernel, n_row, n_col), out_shape=(jax.Sh...]
where the time goes in v4:
time: 49 us; the launch traced here: 48.9 us
  Pallas kernels  45.2 us (92%)
  between operations  2.41 us (5%)
  local copies, waits for them, and re-layouts  1.26 us (3%)
    pallas_call x1, Pallas kernels, on_device(): pl.pallas_call(functools.partial(kernel, n_row, n_col), out_shape=(jax.Sh...  45.2 us
    unnamed x3, local copies, waits for them, and re-layouts  1.26 us

profile of v4, /device:TPU:0, one launch (start us, length us, event | category | flops | bytes accessed | tf_op | source)
XLA Modules:
  0.0 48.9 jit_solution(14956259030385150925)
XLA Ops:
  0.6 45.2 %shard_map.41 = (f32[8,1,16]{2,1,0:T(1,128)}, f32[1,1]{1,0:T(1,128)}) custom-call(bf16[16,128,128]{2,1,0:T(8,128)(2,1)} %bitcast.5, s32[2,8]{1,0:T(2,128)} %bitcast.6), custom_call_target="tpu_custom_call" | custom-call | tf_op jit(solution)/shard_map/pallas_call | solution.py:496
  45.8 0.0 copy-start
  45.8 0.7 %copy-done = f32[8,1,16]{2,1,0:T(1,128)S(1)} copy-done((f32[8,1,16]{2,1,0:T(1,128)S(1)}, f32[8,1,16]{2,1,0:T(1,128)}, u32[]{:S(2)}) %copy-start) | copy-done | bytes 536
  46.5 0.6 %copy.6 = f32[8,1,16]{2,1,0:T(1,128)} copy(f32[8,1,16]{2,1,0:T(1,128)S(1)} %copy-done) | data formatting | bytes 1024
Async XLA Ops:
  45.8 0.7 %copy-start = (f32[8,1,16]{2,1,0:T(1,128)S(1)}, f32[8,1,16]{2,1,0:T(1,128)}, u32[]{:S(2)}) copy-start(f32[8,1,16]{2,1,0:T(1,128)} %get-tuple-element.8) | copy-start | bytes 1540

commit v5 on v4

--- a/solution.py
+++ b/solution.py
@@ -369,9 +369,9 @@
 
     for t in range(2, reach):
         pass_on(t)
+    near_unit(r)
     if moved:
         far_relay(True)
-    near_unit(r)
     for t in range(1, reach):
         units(t)
     far_to_smem = pltpu.make_async_copy(far_idx, far_smem, smem_sem.at[2])

time: 49 us -> 48.9 us (level)
  no operation moved by 1% of the time
where the time goes in v5:
time: 48.9 us; the launch traced here: 48.7 us
  Pallas kernels  45.1 us (92%)
  between operations  2.41 us (5%)
  local copies, waits for them, and re-layouts  1.26 us (3%)
    pallas_call x1, Pallas kernels, on_device(): pl.pallas_call(functools.partial(kernel, n_row, n_col), out_shape=(jax.Sh...  45.1 us
    unnamed x3, local copies, waits for them, and re-layouts  1.26 us

profile of v5, /device:TPU:0, one launch (start us, length us, event | category | flops | bytes accessed | tf_op | source)
XLA Modules:
  0.0 48.7 jit_solution(8664208314691915689)
XLA Ops:
  0.6 45.1 %shard_map.41 = (f32[8,1,16]{2,1,0:T(1,128)}, f32[1,1]{1,0:T(1,128)}) custom-call(bf16[16,128,128]{2,1,0:T(8,128)(2,1)} %bitcast.5, s32[2,8]{1,0:T(2,128)} %bitcast.6), custom_call_target="tpu_custom_call" | custom-call | tf_op jit(solution)/shard_map/pallas_call | solution.py:496
  45.7 0.0 copy-start
  45.7 0.7 %copy-done = f32[8,1,16]{2,1,0:T(1,128)S(1)} copy-done((f32[8,1,16]{2,1,0:T(1,128)S(1)}, f32[8,1,16]{2,1,0:T(1,128)}, u32[]{:S(2)}) %copy-start) | copy-done | bytes 536
  46.4 0.6 %copy.6 = f32[8,1,16]{2,1,0:T(1,128)} copy(f32[8,1,16]{2,1,0:T(1,128)S(1)} %copy-done) | data formatting | bytes 1024
Async XLA Ops:
  45.7 0.7 %copy-start = (f32[8,1,16]{2,1,0:T(1,128)S(1)}, f32[8,1,16]{2,1,0:T(1,128)}, u32[]{:S(2)}) copy-start(f32[8,1,16]{2,1,0:T(1,128)} %get-tuple-element.8) | copy-start | bytes 1540

commit v6 on v5

--- a/solution.py
+++ b/solution.py
@@ -374,21 +374,21 @@
         far_relay(True)
     for t in range(1, reach):
         units(t)
-    far_to_smem = pltpu.make_async_copy(far_idx, far_smem, smem_sem.at[2])
-    if moved:
-        far_relay(False)
-        for e in range(n_far):
-            @pl.when(inner & (far_place(e)[0] != c))
-            def _():
-                far_index(e, 1).wait_recv()
-
-        @pl.when(inner)
-        def _():
-            far_to_smem.start()
     if reach > 1:
         pass_on(reach)
     if reach > 0:
         units(reach)
+    far_to_smem = pltpu.make_async_copy(far_idx, far_smem, smem_sem.at[2])
+    if moved:
+        far_relay(False)
+        for e in range(n_far):
+            @pl.when(inner & (far_place(e)[0] != c))
+            def _():
+                far_index(e, 1).wait_recv()
+
+        @pl.when(inner)
+        def _():
+            far_to_smem.start()
     if moved:
         far_end()
 

time: 48.9 us -> 50.9 us (1.041)
  Pallas kernels: 45.1 us -> 47 us
    pallas_call x1, Pallas kernels: 45.1 us -> 47 us  [on_device(): pl.pallas_call(functools.partial(kernel, n_row, n_col), out_shape=(jax.Sh...]
where the time goes in v6:
time: 50.9 us; the launch traced here: 50.7 us
  Pallas kernels  47 us (92%)
  between operations  2.41 us (5%)
  local copies, waits for them, and re-layouts  1.26 us (2%)
    pallas_call x1, Pallas kernels, on_device(): pl.pallas_call(functools.partial(kernel, n_row, n_col), out_shape=(jax.Sh...  47 us
    unnamed x3, local copies, waits for them, and re-layouts  1.26 us

profile of v6, /device:TPU:0, one launch (start us, length us, event | category | flops | bytes accessed | tf_op | source)
XLA Modules:
  0.0 50.7 jit_solution(12210037238193660406)
XLA Ops:
  0.6 47.0 %shard_map.41 = (f32[8,1,16]{2,1,0:T(1,128)}, f32[1,1]{1,0:T(1,128)}) custom-call(bf16[16,128,128]{2,1,0:T(8,128)(2,1)} %bitcast.5, s32[2,8]{1,0:T(2,128)} %bitcast.6), custom_call_target="tpu_custom_call" | custom-call | tf_op jit(solution)/shard_map/pallas_call | solution.py:496
  47.6 0.0 copy-start
  47.7 0.7 %copy-done = f32[8,1,16]{2,1,0:T(1,128)S(1)} copy-done((f32[8,1,16]{2,1,0:T(1,128)S(1)}, f32[8,1,16]{2,1,0:T(1,128)}, u32[]{:S(2)}) %copy-start) | copy-done | bytes 536
  48.3 0.6 %copy.6 = f32[8,1,16]{2,1,0:T(1,128)} copy(f32[8,1,16]{2,1,0:T(1,128)S(1)} %copy-done) | data formatting | bytes 1024
Async XLA Ops:
  47.6 0.7 %copy-start = (f32[8,1,16]{2,1,0:T(1,128)S(1)}, f32[8,1,16]{2,1,0:T(1,128)}, u32[]{:S(2)}) copy-start(f32[8,1,16]{2,1,0:T(1,128)} %get-tuple-element.8) | copy-start | bytes 1540
